TPU v7x, 32 devices: a whole 2x2x4 slice. The times are simulated.
32 devices in a mesh: groups: 2 (over x), grid: 4 (over y, core), orb: 4 (over z).
Axes of the slice: x: 2, y: 2, z: 4, core: 2. Of those that a mesh axis runs over, the one named last changes fastest.
Arguments:
- orbitals: float32 [32, 2, 128, 128, 128], P(('groups', 'orb'), None, 'grid'), parts along dimension 0, may hold values from -6 to 6
- v_local: float32 [256, 128, 128], P(('groups', 'grid')), parts along dimension 0, may hold values from -24 to 24
- occupations: float32 [32], P('groups'), parts along dimension 0, may hold values from 0.05 to 0.5
Outputs:
- orbitals_next: float32 [32, 2, 128, 128, 128], P(('groups', 'orb'), None, 'grid'), parts along dimension 0
There are 2 independent parts, one for each index of `groups`. A program takes and returns all parts, laid end to end along the dimension named above; each array names one. Nothing has to cross between parts.
All inputs are finite; a program needn't handle non-finite values.
Results may differ from a plain program's by a relative error of at most 0.00035.
Values sent between devices are 32-bit elements; how exact they have to be, the bound alone decides.
A program may use at most 128 MiB of HBM per device.

v0:
```python
from functools import partial
import math

import jax
import jax.numpy as jnp
from jax import lax
from jax.sharding import PartitionSpec as P

TIME_STEP = 0.05
KINETIC_RATE = 0.1
HARTREE_SCALE = math.pi
HIGHEST_PRECISION = lax.Precision.HIGHEST


def apply_along(values, table, axis):
    contracted = jnp.tensordot(values, table, axes=([axis], [0]), precision=HIGHEST_PRECISION)
    return jnp.moveaxis(contracted, -1, axis)


def complex_along(real_part, imag_part, tables, axis):
    table_re, table_im = tables
    new_re = apply_along(real_part, table_re, axis) - apply_along(imag_part, table_im, axis)
    new_im = apply_along(real_part, table_im, axis) + apply_along(imag_part, table_re, axis)
    return (new_re, new_im)


def wave_squared(length):
    mode_ids = jnp.arange(length, dtype=jnp.int32)
    signed = jnp.where(mode_ids < (length + 1) // 2, mode_ids, mode_ids - length)
    wavenumber = 2.0 * math.pi * signed.astype(jnp.float32) / length
    return wavenumber * wavenumber


def mode_angles(length):
    mode_ids = jnp.arange(length, dtype=jnp.int32)
    product = mode_ids[:, None] * mode_ids[None, :] % length
    return 2.0 * math.pi * product.astype(jnp.float32) / length


def forward_table(length):
    phase_angle = mode_angles(length)
    return (jnp.cos(phase_angle), -jnp.sin(phase_angle))


def inverse_table(length):
    phase_angle = mode_angles(length)
    return (jnp.cos(phase_angle) / length, jnp.sin(phase_angle) / length)


def matmul_high(left, right):
    return jnp.dot(left, right, precision=HIGHEST_PRECISION)


def kinetic_table(length):
    inv_re, inv_im = inverse_table(length)
    fwd_re, fwd_im = forward_table(length)
    kinetic_turn = -KINETIC_RATE * wave_squared(length)
    phase_re = jnp.cos(kinetic_turn)[None, :]
    phase_im = jnp.sin(kinetic_turn)[None, :]
    left_re = inv_re * phase_re - inv_im * phase_im
    left_im = inv_re * phase_im + inv_im * phase_re
    table_re = matmul_high(left_re, fwd_re) - matmul_high(left_im, fwd_im)
    table_im = matmul_high(left_re, fwd_im) + matmul_high(left_im, fwd_re)
    return (table_re, table_im)


def coulomb_kernel(squares_x, squares_y, squares_z):
    total = squares_x[:, None, None] + squares_y[None, :, None] + squares_z[None, None, :]
    anchor = total <= 0.0
    return jnp.where(anchor, 0.0, HARTREE_SCALE / jnp.where(anchor, 1.0, total))


def kinetic_local(orbitals):
    count_y = orbitals.shape[3]
    count_z = orbitals.shape[4]
    real_part, imag_part = (orbitals[:, 0], orbitals[:, 1])
    real_part, imag_part = complex_along(real_part, imag_part, kinetic_table(count_z), 3)
    real_part, imag_part = complex_along(real_part, imag_part, kinetic_table(count_y), 2)
    return jnp.stack([real_part, imag_part], 1)


def kinetic_across(received, table_x):
    blocks = received.shape[0]
    planes = received.shape[3]
    kernel_re = table_x[0].reshape(blocks, planes, blocks, planes)
    kernel_im = table_x[1].reshape(blocks, planes, blocks, planes)
    contract = partial(jnp.einsum, "glxyz,gxhv->hlvyz", precision=HIGHEST_PRECISION)
    real_part = received[:, :, 0]
    imag_part = received[:, :, 1]
    out_re = contract(real_part, kernel_re) - contract(imag_part, kernel_im)
    out_im = contract(real_part, kernel_im) + contract(imag_part, kernel_re)
    return jnp.stack([out_re, out_im], 2)


def rotate_phase(real_part, imag_part, field):
    phase_angle = TIME_STEP * field
    cosine = jnp.cos(phase_angle)
    sine = jnp.sin(phase_angle)
    return (real_part * cosine + imag_part * sine, imag_part * cosine - real_part * sine)


def real_forward(density, axis):
    table_re, table_im = forward_table(density.shape[axis])
    return (apply_along(density, table_re, axis), apply_along(density, table_im, axis))


def real_inverse(real_part, imag_part, axis):
    table_re, table_im = inverse_table(real_part.shape[axis])
    return apply_along(real_part, table_re, axis) - apply_along(imag_part, table_im, axis)


def poisson_shared(density):
    width_x, block_y, count_z = density.shape
    span_count = lax.axis_size("grid") * lax.axis_size("orb")
    block_x = width_x // span_count
    real_part, imag_part = real_forward(density, 2)
    real_part, imag_part = complex_along(real_part, imag_part, forward_table(width_x), 0)
    spread = lax.all_to_all(
        jnp.stack([real_part, imag_part], 0),
        ("grid", "orb"),
        split_axis=1,
        concat_axis=2,
        tiled=True,
    )
    count_y = spread.shape[2]
    real_part, imag_part = complex_along(spread[0], spread[1], forward_table(count_y), 1)
    start_x = lax.axis_index(("grid", "orb")) * block_x
    squares_x = lax.dynamic_slice_in_dim(wave_squared(width_x), start_x, block_x, 0)
    kernel = coulomb_kernel(squares_x, wave_squared(count_y), wave_squared(count_z))
    real_part, imag_part = complex_along(
        real_part * kernel, imag_part * kernel, inverse_table(count_y), 1
    )
    back = lax.all_to_all(
        jnp.stack([real_part, imag_part], 0),
        ("grid", "orb"),
        split_axis=2,
        concat_axis=1,
        tiled=True,
    )
    real_part, imag_part = complex_along(back[0], back[1], inverse_table(width_x), 0)
    return real_inverse(real_part, imag_part, 2)


def body(orbitals, v_local, occupations):
    layers = orbitals.shape[0]
    planes = orbitals.shape[2]
    count_y = orbitals.shape[3]
    count_z = orbitals.shape[4]
    grid_count = lax.axis_size("grid")
    width_x = planes * grid_count
    table_x = kinetic_table(width_x)
    local = kinetic_local(orbitals)[None]
    orb_count = lax.axis_size("orb")
    received = lax.all_to_all(local, "grid", split_axis=4, concat_axis=0, tiled=True)
    moved = kinetic_across(received, table_x)
    returned = lax.all_to_all(moved, "grid", split_axis=0, concat_axis=4, tiled=True)[0]
    weights = lax.dynamic_slice_in_dim(occupations, lax.axis_index("orb") * layers, layers, 0)
    squares = returned[:, 0] * returned[:, 0] + returned[:, 1] * returned[:, 1]
    partial_density = jnp.einsum("l,lxyz->xyz", weights, squares, precision=HIGHEST_PRECISION)
    share_y = count_y // (grid_count * orb_count)
    reordered = partial_density.reshape(planes, grid_count, orb_count, share_y, count_z)
    reordered = reordered.transpose(0, 2, 1, 3, 4).reshape(planes, count_y, count_z)
    share = lax.psum_scatter(reordered, "orb", scatter_dimension=1, tiled=True)
    lines = lax.all_to_all(share, "grid", split_axis=1, concat_axis=0, tiled=True)
    hartree_lines = poisson_shared(lines)
    rows_back = lax.all_to_all(hartree_lines, "grid", split_axis=0, concat_axis=1, tiled=True)
    gathered = lax.all_gather(rows_back, "orb", axis=1, tiled=True)
    hartree = gathered.reshape(planes, orb_count, grid_count, share_y, count_z)
    hartree = hartree.transpose(0, 2, 1, 3, 4).reshape(planes, count_y, count_z)
    new_re, new_im = rotate_phase(returned[:, 0], returned[:, 1], v_local + hartree)
    return jnp.stack([new_re, new_im], 1)


def solution(mesh):
    return jax.shard_map(
        body,
        mesh=mesh,
        in_specs=(
            P(("groups", "orb"), None, "grid", None, None),
            P(("groups", "grid"), None, None),
            P("groups"),
        ),
        out_specs=P(("groups", "orb"), None, "grid", None, None),
        check_vma=False,
    )
```

profile of v0, /device:TPU:0, one launch (start us, length us, event | category | flops | bytes accessed | tf_op | source)
XLA Modules:
  0.0 829.5 jit_solution(16767889140726993420)
XLA Ops:
  8.0 10.1 %fusion = f32[128,4,32,128]{3,0,2,1:T(8,128)S(1)} fusion(f32[4,2,32,128,128]{4,3,2,1,0:T(8,128)} %param.3, f32[128,128]{1,0:T(8,128)S(1)} %convolution_subtract_fusion.5), kind=kOutput, calls=%fused_computation.6 | convolution fusion | flops 3221225472 | bytes 16842752 | tf_op jit(solution)/shard_map/dot_general | solution.py:16
  18.2 10.6 %fusion.6 = f32[128,4,32,128]{3,0,2,1:T(8,128)S(1)} fusion(f32[4,2,32,128,128]{4,3,2,1,0:T(8,128)} %param.3, f32[128,128]{1,0:T(8,128)S(1)} %convolution_subtract_fusion.5), kind=kOutput, calls=%fused_computation.12 | convolution fusion | flops 3221225472 | bytes 16842752 | tf_op jit(solution)/shard_map/dot_general | solution.py:16
  29.2 10.8 %fusion.4 = f32[128,4,32,128]{3,0,2,1:T(8,128)S(1)} fusion(f32[4,2,32,128,128]{4,3,2,1,0:T(8,128)} %param.3, f32[128,128]{1,0:T(8,128)S(1)} %convolution_add_fusion.4), kind=kOutput, calls=%fused_computation.10 | convolution fusion | flops 3221225472 | bytes 16842752 | tf_op jit(solution)/shard_map/dot_general | solution.py:16
  40.0 12.1 %fusion.2 = f32[128,4,32,128]{3,0,2,1:T(8,128)} fusion(f32[4,2,32,128,128]{4,3,2,1,0:T(8,128)} %param.3, f32[128,128]{1,0:T(8,128)S(1)} %convolution_add_fusion.4), kind=kOutput, calls=%fused_computation.8 | convolution fusion | flops 3221225472 | bytes 16842752 | tf_op jit(solution)/shard_map/dot_general | solution.py:16
  52.0 8.9 %fusion.10 = f32[4,32,128,128]{3,2,1,0:T(8,128)} fusion(f32[128,4,32,128]{3,0,2,1:T(8,128)S(1)} %fusion.4, f32[128,4,32,128]{3,0,2,1:T(8,128)S(1)} %fusion, f32[128,128]{1,0:T(8,128)S(1)} %convolution_subtract_fusion.5), kind=kOutput, calls=%fused_computation.18 | convolution fusion | flops 3223322624 | bytes 25231360 | tf_op jit(solution)/shard_map/dot_general | solution.py:16
  61.0 9.1 %fusion.12 = f32[4,32,128,128]{3,2,1,0:T(8,128)} fusion(f32[128,4,32,128]{3,0,2,1:T(8,128)S(1)} %fusion.4, f32[128,4,32,128]{3,0,2,1:T(8,128)S(1)} %fusion, f32[128,128]{1,0:T(8,128)S(1)} %convolution_add_fusion.4), kind=kOutput, calls=%fused_computation.20 | convolution fusion | flops 3223322624 | bytes 25231360 | tf_op jit(solution)/shard_map/dot_general | solution.py:16
  70.1 13.4 %add_bitcast_fusion = f32[4,1,32,128,128]{3,4,2,0,1:T(8,128)} fusion(f32[4,32,128,128]{3,2,1,0:T(8,128)} %fusion.10, f32[128,4,32,128]{3,0,2,1:T(8,128)S(1)} %fusion.6, f32[128,4,32,128]{3,0,2,1:T(8,128)} %fusion.2, f32[128,128]{1,0:T(8,128)S(1)} %convolution_add_fusion.4), kind=kOutput, calls=%fused_computation.31 | convolution fusion | flops 3225419776 | bytes 33619968 | tf_op jit(solution)/shard_map/dot_general | solution.py:16
  83.5 11.4 %subtract_bitcast_fusion = f32[4,1,32,128,128]{3,4,2,0,1:T(8,128)} fusion(f32[4,32,128,128]{3,2,1,0:T(8,128)S(1)} %copy-done.2, f32[128,4,32,128]{3,0,2,1:T(8,128)S(1)} %fusion.6, f32[128,4,32,128]{3,0,2,1:T(8,128)} %fusion.2, f32[128,128]{1,0:T(8,128)S(1)} %convolution_subtract_fusion.5), kind=kOutput, calls=%fused_computation.32 | convolution fusion | flops 3225419776 | bytes 33619968 | tf_op jit(solution)/shard_map/dot_general | solution.py:16
  94.9 11.9 %maximum_bitcast_fusion = f32[1,4,2,32,128,128]{4,5,3,1,2,0:T(8,128)} fusion(f32[4,1,32,128,128]{3,4,2,0,1:T(8,128)} %add_bitcast_fusion, f32[4,1,32,128,128]{3,4,2,0,1:T(8,128)} %subtract_bitcast_fusion), kind=kLoop, calls=%fused_computation | loop fusion | flops 4194304 | bytes 33554432 | tf_op jit(solution)/shard_map/broadcast_in_dim | solution.py:152
  106.8 19.9 %copy.131 = f32[1,4,2,32,128,128]{5,3,1,2,0,4:T(8,128)} copy(f32[1,4,2,32,128,128]{4,5,3,1,2,0:T(8,128)} %maximum_bitcast_fusion) | data formatting | bytes 33554432 | tf_op jit(solution)/shard_map/broadcast_in_dim | solution.py:152
  126.7 7.0 all-to-all-start
  134.3 183.0 %all-to-all-done = f32[1,4,2,32,128,128]{5,3,1,2,0,4:T(8,128)} async-done(((f32[1,4,2,32,128,128]{5,3,1,2,0,4:T(8,128)}), f32[1,4,2,32,128,128]{5,3,1,2,0,4:T(8,128)}, u32[]{:S(2)}, u32[]{:S(2)}) %all-to-all-start) | async-done | bytes 16777248 | tf_op jit(solution)/shard_map/all_to_all | solution.py:154
  317.4 7.4 copy.253
  324.8 7.8 fusion.20
  332.6 8.0 fusion.21
  340.6 10.1 %fusion.8 = f32[4,4,1,32,32,128]{5,3,4,1,0,2:T(8,128)} fusion(f32[4,32,4,32,128,1]{4,1,5,3,2,0:T(8,128)S(1)} %fusion.20, f32[4,32,4,32,1,1]{1,3,0,5,4,2:T(8,128)S(1)} %copy.176, f32[4,4,2,32,32,128]{5,3,0,4,1,2:T(8,128)S(1)} %bitcast.263), kind=kOutput, calls=%fused_computation.15 | convolution fusion | flops 3223322624 | bytes 25427968 | tf_op jit(solution)/shard_map/glxyz,gxhv->hlvyz/dot_general | solution.py:91
  350.7 10.1 %fusion.9 = f32[4,4,1,32,32,128]{5,3,4,1,0,2:T(8,128)} fusion(f32[4,32,4,32,128,1]{4,1,5,3,2,0:T(8,128)S(1)} %fusion.21, f32[4,32,4,32,1,1]{1,3,0,5,4,2:T(8,128)S(1)} %copy.178, f32[4,4,2,32,32,128]{5,3,0,4,1,2:T(8,128)S(1)} %bitcast.264), kind=kOutput, calls=%fused_computation.17 | convolution fusion | flops 3223322624 | bytes 25427968 | tf_op jit(solution)/shard_map/glxyz,gxhv->hlvyz/dot_general | solution.py:90
  360.8 5.1 pad_maximum_fusion
  366.0 7.5 copy.138
  373.5 7.0 all-to-all-start.1
  380.5 183.0 %all-to-all-done.1 = f32[4,4,2,32,32,128]{5,3,4,1,2,0:T(8,128)} async-done(((f32[4,4,2,32,32,128]{5,3,4,1,2,0:T(8,128)}), f32[4,4,2,32,32,128]{5,3,4,1,2,0:T(8,128)}, u32[]{:S(2)}, u32[]{:S(2)}) %all-to-all-start.1) | async-done | bytes 16777248 | tf_op jit(solution)/shard_map/all_to_all | solution.py:156
  563.5 15.4 %copy.139 = f32[4,4,2,32,32,128]{5,4,0,3,2,1:T(8,128)S(1)} copy(f32[4,4,2,32,32,128]{5,3,4,1,2,0:T(8,128)} %all-to-all-done.1) | data formatting | bytes 33554432 | tf_op jit(solution)/shard_map/all_to_all | solution.py:156
  581.5 3.9 copy-done.1
  585.4 18.1 %fusion.18 = f32[1,32,4,4,8,128]{5,0,4,3,2,1:T(1,128)S(1)} fusion(f32[32,4,4,8,128,4]{4,3,2,1,0,5:T(8,128)S(1)} %bitcast.267, f32[16]{0:T(128)S(1)} %copy-done, s32[]{:T(128)S(6)} %select_n.134), kind=kOutput, calls=%fused_computation.26 | convolution fusion | flops 25165824 | bytes 10485828 | tf_op jit(solution)/shard_map/l,lxyz->xyz/dot_general | solution.py:159
  605.1 44.9 %reduce-scatter.2.cloned.1.call-done = f32[32,32,128]{2,1,0:T(8,128)} async-done(((f32[32,128,128]{2,1,0:T(8,128)}), f32[32,32,128]{2,1,0:T(8,128)}) %reduce-scatter.2.cloned.1.call-update) | async-done | bytes 524304 | tf_op jit(solution)/shard_map/reduce_scatter | solution.py:163
  651.3 11.8 %all_to_all.99 = f32[32,32,128]{2,0,1:T(8,128)S(1)} all-to-all(f32[32,32,128]{2,0,1:T(8,128)S(1)} %copy.140), channel_id=1, replica_groups=mesh['groups'=2,'grid'=4,'orb'=4] {'grid'}, dimensions={1} | all-to-all | bytes 1048576 | tf_op jit(solution)/shard_map/all_to_all | solution.py:164
  674.0 26.4 %all-to-all-done.3 = f32[2,128,8,128]{3,2,0,1:T(8,128)S(1)} async-done(((f32[2,128,8,128]{3,2,0,1:T(8,128)}), f32[2,128,8,128]{3,2,0,1:T(8,128)S(1)}, u32[]{:S(2)}, u32[]{:S(2)}) %all-to-all-start.3) | async-done | bytes 1048608 | tf_op jit(solution)/shard_map/all_to_all | solution.py:118
  709.3 30.2 %all_to_all.100 = f32[2,8,128,128]{3,1,0,2:T(8,128)S(1)} all-to-all(f32[2,8,128,128]{3,1,0,2:T(8,128)S(1)} %copy.155), channel_id=1, replica_groups=mesh['groups'=2,'grid'=4,'orb'=4] {'grid','orb'}, dimensions={2} | all-to-all | bytes 2097152 | tf_op jit(solution)/shard_map/all_to_all | solution.py:133
  745.6 11.2 %all_to_all.101 = f32[128,8,128]{2,1,0:T(8,128)S(1)} all-to-all(f32[128,8,128]{2,1,0:T(8,128)S(1)} %copy.167), channel_id=1, replica_groups=mesh['groups'=2,'grid'=4,'orb'=4] {'grid'}, dimensions={0} | all-to-all | bytes 1048576 | tf_op jit(solution)/shard_map/all_to_all | solution.py:166
  757.7 43.7 %all-gather.2.cloned.1.call-done = f32[32,128,128]{2,1,0:T(8,128)} async-done(((f32[32,32,128]{2,1,0:T(8,128)}), f32[32,128,128]{2,1,0:T(8,128)}) %all-gather.2.cloned.1.call-update) | async-done | bytes 2097168 | tf_op jit(solution)/shard_map/all_gather | solution.py:167
  803.3 7.7 fusion.46
  811.0 11.3 %multiply_add_fusion = (f32[4,2,32,128,128]{4,3,2,1,0:T(8,128)}, f32[4,2,32,128,128]{4,3,2,1,0:T(8,128)}) fusion(f32[4,2,32,128,128]{4,3,2,1,0:T(8,128)} %bitcast.266, f32[32,128,128]{2,1,0:T(8,128)S(1)} %get-tuple-element.8, f32[32,128,128]{2,1,0:T(8,128)S(1)} %get-tuple-element.7, ...), kind=kLoop, output_to_operand_aliasing={{0}: (3, {}), {1}: (3, {})}, calls=%fused_computation.29 | loop fusion | flops 12582912 | bytes 37748736 | tf_op jit(solution)/shard_map/add | solution.py:99
  (64 shorter events, 36.4 us)
Async XLA Ops:
  6.5 578.8 %copy-start = (f32[16]{0:T(128)S(1)}, f32[16]{0:T(128)}, u32[]{:S(2)}) copy-start(f32[16]{0:T(128)} %param.5) | copy-start | bytes 196
  70.1 13.4 %copy-start.2 = (f32[4,32,128,128]{3,2,1,0:T(8,128)S(1)}, f32[4,32,128,128]{3,2,1,0:T(8,128)}, u32[]{:S(2)}) copy-start(f32[4,32,128,128]{3,2,1,0:T(8,128)} %fusion.12) | copy-start | bytes 25165828
  126.7 190.7 %all-to-all-start = ((f32[1,4,2,32,128,128]{5,3,1,2,0,4:T(8,128)}), f32[1,4,2,32,128,128]{5,3,1,2,0,4:T(8,128)}, u32[]{:S(2)}, u32[]{:S(2)}) async-start(f32[1,4,2,32,128,128]{5,3,1,2,0,4:T(8,128)} %copy.131), calls=%async_computation | async-start | bytes 33554432 | tf_op jit(solution)/shard_map/all_to_all | solution.py:154
  350.7 10.1 %copy-start.3 = (f32[4,4,1,32,32,128]{5,3,4,1,0,2:T(8,128)S(1)}, f32[4,4,1,32,32,128]{5,3,4,1,0,2:T(8,128)}, u32[]{:S(2)}) copy-start(f32[4,4,1,32,32,128]{5,3,4,1,0,2:T(8,128)} %fusion.8) | copy-start | bytes 25165828
  373.5 190.0 %all-to-all-start.1 = ((f32[4,4,2,32,32,128]{5,3,4,1,2,0:T(8,128)}), f32[4,4,2,32,32,128]{5,3,4,1,2,0:T(8,128)}, u32[]{:S(2)}, u32[]{:S(2)}) async-start(f32[4,4,2,32,32,128]{5,3,4,1,2,0:T(8,128)} %copy.138), calls=%async_computation.1 | async-start | bytes 33554432 | tf_op jit(solution)/shard_map/all_to_all | solution.py:156
  380.5 269.5 %reduce-scatter.2.cloned.1.call-start = ((), (), s32[]{:S(2)}) async-start(), calls=%async_computation.7 | async-start | bytes 2621440 | tf_op jit(solution)/shard_map/reduce_scatter | solution.py:163
  578.9 6.4 copy-start.1
  670.0 30.5 %all-to-all-start.3 = ((f32[2,128,8,128]{3,2,0,1:T(8,128)}), f32[2,128,8,128]{3,2,0,1:T(8,128)S(1)}, u32[]{:S(2)}, u32[]{:S(2)}) async-start(f32[2,128,8,128]{3,2,0,1:T(8,128)} %copy.147), calls=%async_computation.4 | async-start | bytes 2097152 | tf_op jit(solution)/shard_map/all_to_all | solution.py:118
  673.6 127.8 %all-gather.2.cloned.1.call-start = ((), (), s32[]{:S(2)}) async-start(), calls=%async_computation.8 | async-start | bytes 2621440 | tf_op jit(solution)/shard_map/all_gather | solution.py:167
  740.0 63.3 %copy-start.4 = (f32[32,128,128]{2,1,0:T(8,128)S(1)}, f32[32,128,128]{2,1,0:T(8,128)}, u32[]{:S(2)}) copy-start(f32[32,128,128]{2,1,0:T(8,128)} %param.4) | copy-start | bytes 6291460
Sparse Core Ops, SparseCore 0:
  605.2 44.7 reduce-scatter.1
  757.8 43.5 all-gather.1
where the time goes:
time: 837 us; the launch traced here: 829 us
  waiting for transfers between devices  481 us (57%)
  matrix products  161 us (19%)
  local copies, waits for them, and re-layouts  63.7 us (8%)
  blocking collectives  53.2 us (6%)
  other arithmetic  38.9 us (5%)
  starting transfers between devices  17.9 us (2%)
  between operations  14.1 us (2%)
    all_to_all x1, waiting for transfers between devices, body(): lax.all_to_all(local, 'grid', split_axis=4, concat_axis=0, tiled=True)  183 us
    all_to_all x1, waiting for transfers between devices, body(): lax.all_to_all(moved, 'grid', split_axis=0, concat_axis=4, tiled=True)[0]  183 us
    dot_general x28, matrix products, apply_along(): jnp.tensordot(values, table, axes=([axis], [0]), precision=HIGHEST_PRECIS...  105 us
    reduce_scatter x1, waiting for transfers between devices, body(): share = lax.psum_scatter(reordered, 'orb', scatter_dimension=1, tiled=True)  44.9 us
    all_gather x1, waiting for transfers between devices, body(): gathered = lax.all_gather(rows_back, 'orb', axis=1, tiled=True)  43.7 us
    all_to_all x1, blocking collectives, poisson_shared(): lax.all_to_all(jnp.stack([real_part, imag_part], 0), ('grid', 'orb'), spl...  30.2 us
    all_to_all x1, waiting for transfers between devices, poisson_shared(): lax.all_to_all(jnp.stack([real_part, imag_part], 0), ('grid', 'orb'), spl...  26.4 us
    broadcast_in_dim x1, local copies, waits for them, and re-layouts, body(): local = kinetic_local(orbitals)[None]  19.9 us
  transfers between devices with their start and end apart: 5, of which 5 were waited for; matrix products, arithmetic and copies ran while one was open for 0% of the time, Pallas kernels for 0%

commit v1 on v0

v1 whole, which is shorter than its diff:
```python
from functools import partial
import math

import jax
import jax.numpy as jnp
import ml_dtypes
import numpy as np
from jax import lax
from jax.experimental import pallas as pl
from jax.experimental.pallas import tpu as pltpu
from jax.sharding import PartitionSpec as P

TIME_STEP = 0.05
KINETIC_RATE = 0.1
HARTREE_SCALE = math.pi
HIGHEST = lax.Precision.HIGHEST
VMEM_LIMIT = 50 * 1024 * 1024


def wave_squared(length):
    ids = np.arange(length)
    signed = np.where(ids < (length + 1) // 2, ids, ids - length)
    return (2.0 * np.pi * signed / length) ** 2


def fourier(length, sign):
    ids = np.arange(length)
    return np.exp(sign * 2j * np.pi * ((ids[:, None] * ids[None, :]) % length) / length)


def kinetic_matrix(length):
    phase = np.exp(-1j * KINETIC_RATE * wave_squared(length))
    return (fourier(length, 1) / length * phase[None, :]) @ fourier(length, -1)


def left_block(matrix):
    return np.block([[matrix.real, -matrix.imag], [matrix.imag, matrix.real]])


def right_block(matrix):
    return np.block([[matrix.real, matrix.imag], [-matrix.imag, matrix.real]])


def split_const(table):
    table = np.asarray(table, np.float32)
    high = table.astype(ml_dtypes.bfloat16)
    low = (table - high.astype(np.float32)).astype(ml_dtypes.bfloat16)
    return np.stack([high, low])


def split(values):
    high = values.astype(jnp.bfloat16)
    low = (values - high.astype(jnp.float32)).astype(jnp.bfloat16)
    return high, low


def dot(left, right):
    return jnp.dot(left, right, preferred_element_type=jnp.float32)


def data_by_table(values, table):
    high, low = split(values)
    return dot(high, table[0]) + dot(high, table[1]) + dot(low, table[0])


def table_by_data(table, values):
    high, low = split(values)
    return dot(table[0], high) + dot(table[1], high) + dot(table[0], low)


def local_kernel(psi_ref, wz_ref, wy_ref, out_ref):
    _, _, bx, ny, nz = psi_ref.shape
    grid_count, _, _, vy, _ = out_ref.shape
    real_part = psi_ref[0, 0].reshape(bx * ny, nz)
    imag_part = psi_ref[0, 1].reshape(bx * ny, nz)
    turned = data_by_table(jnp.concatenate([real_part, imag_part], 1), wz_ref)
    columns = [
        jnp.concatenate(
            [turned[p * ny : (p + 1) * ny, :nz], turned[p * ny : (p + 1) * ny, nz:]], 0
        )
        for p in range(bx)
    ]
    rows = table_by_data(wy_ref, jnp.concatenate(columns, 1))
    for g in range(grid_count):
        for c in range(2):
            start = c * ny + g * vy
            for p in range(bx):
                out_ref[g, c, p] = rows[start : start + vy, p * nz : (p + 1) * nz]


def kinetic_local(orbitals, layer, grid_count, wz, wy):
    _, _, planes, ny, nz = orbitals.shape
    bx = min(4, planes)
    vy = ny // grid_count
    return pl.pallas_call(
        local_kernel,
        grid=(planes // bx,),
        in_specs=[
            pl.BlockSpec((1, 2, bx, ny, nz), lambda i: (layer, 0, i, 0, 0)),
            pl.BlockSpec(wz.shape, lambda i: (0, 0, 0)),
            pl.BlockSpec(wy.shape, lambda i: (0, 0, 0)),
        ],
        out_specs=pl.BlockSpec((grid_count, 2, bx, vy, nz), lambda i: (0, 0, i, 0, 0)),
        out_shape=jax.ShapeDtypeStruct((grid_count, 2, planes, vy, nz), jnp.float32),
        compiler_params=pltpu.CompilerParams(vmem_limit_bytes=VMEM_LIMIT),
        cost_estimate=pl.CostEstimate(
            flops=3 * 8 * planes * ny * nz * (ny + nz),
            bytes_accessed=16 * planes * ny * nz,
            transcendentals=0,
        ),
    )(orbitals, wz, wy)


def across_kernel(planes, first, weight_ref, psi_ref, wx_ref, *refs):
    if first:
        out_ref, density_ref = refs
    else:
        earlier_ref, out_ref, density_ref = refs
    depth, by, nz = psi_ref.shape
    columns = jnp.concatenate([psi_ref[:, j, :] for j in range(by)], 1)
    moved = table_by_data(wx_ref, columns)
    squares = moved * moved
    weight = weight_ref[0]
    for j in range(by):
        out_ref[:, j, :] = moved[:, j * nz : (j + 1) * nz]
    for h in range(depth // (2 * planes)):
        low = 2 * h * planes
        term = weight * (squares[low : low + planes] + squares[low + planes : low + 2 * planes])
        for j in range(by):
            value = term[:, j * nz : (j + 1) * nz]
            if not first:
                value = value + earlier_ref[h * planes : (h + 1) * planes, j, :]
            density_ref[h * planes : (h + 1) * planes, j, :] = value


def kinetic_across(received, weight, density, wx):
    grid_count, _, planes, vy, nz = received.shape
    depth = grid_count * 2 * planes
    by = min(8, vy)
    first = density is None
    block = pl.BlockSpec((depth, by, nz), lambda i: (0, i, 0))
    density_block = pl.BlockSpec((depth // 2, by, nz), lambda i: (0, i, 0))
    in_specs = [
        pl.BlockSpec(memory_space=pltpu.SMEM),
        block,
        pl.BlockSpec(wx.shape, lambda i: (0, 0, 0)),
    ]
    operands = [weight, received.reshape(depth, vy, nz), wx]
    if not first:
        in_specs.append(density_block)
        operands.append(density)
    moved, density = pl.pallas_call(
        partial(across_kernel, planes, first),
        grid=(vy // by,),
        in_specs=in_specs,
        out_specs=[block, density_block],
        out_shape=[
            jax.ShapeDtypeStruct((depth, vy, nz), jnp.float32),
            jax.ShapeDtypeStruct((depth // 2, vy, nz), jnp.float32),
        ],
        compiler_params=pltpu.CompilerParams(vmem_limit_bytes=VMEM_LIMIT),
        cost_estimate=pl.CostEstimate(
            flops=3 * 2 * depth * depth * vy * nz,
            bytes_accessed=12 * depth * vy * nz,
            transcendentals=0,
        ),
    )(*operands)
    return moved.reshape(grid_count, 2, planes, vy, nz), density


def rotate_kernel(layers, *refs):
    cos_ref, sin_ref = refs[layers], refs[layers + 1]
    out_ref = refs[layers + 2]
    grid_count, _, _, vy, _ = refs[0].shape
    for g in range(grid_count):
        band = slice(g * vy, (g + 1) * vy)
        cosine = cos_ref[:, band, :]
        sine = sin_ref[:, band, :]
        for l in range(layers):
            real_part = refs[l][g, 0]
            imag_part = refs[l][g, 1]
            out_ref[l, 0, :, band, :] = real_part * cosine + imag_part * sine
            out_ref[l, 1, :, band, :] = imag_part * cosine - real_part * sine


def rotate(returned, cosine, sine):
    layers = len(returned)
    grid_count, _, planes, vy, nz = returned[0].shape
    ny = grid_count * vy
    bx = min(4, planes)
    field_block = pl.BlockSpec((bx, ny, nz), lambda i: (i, 0, 0))
    return pl.pallas_call(
        partial(rotate_kernel, layers),
        grid=(planes // bx,),
        in_specs=[pl.BlockSpec((grid_count, 2, bx, vy, nz), lambda i: (0, 0, i, 0, 0))] * layers
        + [field_block, field_block],
        out_specs=pl.BlockSpec((layers, 2, bx, ny, nz), lambda i: (0, 0, i, 0, 0)),
        out_shape=jax.ShapeDtypeStruct((layers, 2, planes, ny, nz), jnp.float32),
        compiler_params=pltpu.CompilerParams(vmem_limit_bytes=VMEM_LIMIT),
    )(*returned, cosine, sine)


def table_of(matrix):
    return (np.asarray(matrix.real, np.float32), np.asarray(matrix.imag, np.float32))


def apply_along(values, table, axis):
    contracted = jnp.tensordot(values, table, axes=([axis], [0]), precision=HIGHEST)
    return jnp.moveaxis(contracted, -1, axis)


def complex_along(real_part, imag_part, matrix, axis):
    table_re, table_im = table_of(matrix)
    new_re = apply_along(real_part, table_re, axis) - apply_along(imag_part, table_im, axis)
    new_im = apply_along(real_part, table_im, axis) + apply_along(imag_part, table_re, axis)
    return (new_re, new_im)


def coulomb_kernel(squares_x, squares_y, squares_z):
    total = squares_x[:, None, None] + squares_y[None, :, None] + squares_z[None, None, :]
    anchor = total <= 0.0
    return jnp.where(anchor, 0.0, HARTREE_SCALE / jnp.where(anchor, 1.0, total))


def poisson_shared(density):
    width_x, _, count_z = density.shape
    span_count = lax.axis_size("grid") * lax.axis_size("orb")
    block_x = width_x // span_count
    forward_z = table_of(fourier(count_z, -1))
    real_part, imag_part = (apply_along(density, forward_z[0], 2), apply_along(density, forward_z[1], 2))
    real_part, imag_part = complex_along(real_part, imag_part, fourier(width_x, -1), 0)
    spread = lax.all_to_all(
        jnp.stack([real_part, imag_part], 0),
        ("grid", "orb"),
        split_axis=1,
        concat_axis=2,
        tiled=True,
    )
    count_y = spread.shape[2]
    real_part, imag_part = complex_along(spread[0], spread[1], fourier(count_y, -1), 1)
    start_x = lax.axis_index(("grid", "orb")) * block_x
    squares_x = lax.dynamic_slice_in_dim(
        jnp.asarray(wave_squared(width_x), jnp.float32), start_x, block_x, 0
    )
    kernel = coulomb_kernel(
        squares_x,
        np.asarray(wave_squared(count_y), np.float32),
        np.asarray(wave_squared(count_z), np.float32),
    )
    real_part, imag_part = complex_along(
        real_part * kernel, imag_part * kernel, fourier(count_y, 1) / count_y, 1
    )
    back = lax.all_to_all(
        jnp.stack([real_part, imag_part], 0),
        ("grid", "orb"),
        split_axis=2,
        concat_axis=1,
        tiled=True,
    )
    real_part, imag_part = complex_along(back[0], back[1], fourier(width_x, 1) / width_x, 0)
    inverse_z = table_of(fourier(count_z, 1) / count_z)
    return apply_along(real_part, inverse_z[0], 2) - apply_along(imag_part, inverse_z[1], 2)


def body(orbitals, v_local, occupations):
    layers, _, planes, count_y, count_z = orbitals.shape
    grid_count = lax.axis_size("grid")
    orb_count = lax.axis_size("orb")
    width_x = planes * grid_count
    share_y = count_y // (grid_count * orb_count)
    wz = jnp.asarray(split_const(right_block(kinetic_matrix(count_z))))
    wy = jnp.asarray(split_const(left_block(kinetic_matrix(count_y))))
    order = np.arange(2 * width_x).reshape(2, grid_count, planes).transpose(1, 0, 2).reshape(-1)
    wx = jnp.asarray(split_const(left_block(kinetic_matrix(width_x))[order][:, order]))
    weights = lax.dynamic_slice_in_dim(occupations, lax.axis_index("orb") * layers, layers, 0)
    exchange = partial(lax.all_to_all, axis_name="grid", split_axis=0, concat_axis=0, tiled=True)

    received = [
        exchange(kinetic_local(orbitals, layer, grid_count, wz, wy)) for layer in range(layers)
    ]
    density = None
    returned = []
    for layer in range(layers):
        moved, density = kinetic_across(
            received[layer], weights[layer : layer + 1], density, wx
        )
        returned.append(exchange(moved))
    share = lax.psum_scatter(density, "orb", scatter_dimension=1, tiled=True)
    share, returned[0] = lax.optimization_barrier((share, returned[0]))
    hartree_lines = poisson_shared(share)
    rows_back = lax.all_to_all(hartree_lines, "grid", split_axis=0, concat_axis=1, tiled=True)
    gathered = lax.all_gather(rows_back, "orb", axis=0, tiled=False)
    hartree = gathered.reshape(orb_count, planes, grid_count, share_y, count_z)
    hartree = hartree.transpose(1, 2, 0, 3, 4).reshape(planes, count_y, count_z)
    angle = TIME_STEP * (v_local + hartree)
    return rotate(returned, jnp.cos(angle), jnp.sin(angle))


def solution(mesh):
    return jax.shard_map(
        body,
        mesh=mesh,
        in_specs=(
            P(("groups", "orb"), None, "grid", None, None),
            P(("groups", "grid"), None, None),
            P("groups"),
        ),
        out_specs=P(("groups", "orb"), None, "grid", None, None),
        check_vma=False,
    )
```

time: 837 us -> 568 us (0.68)
  waiting for transfers between devices: 481 us -> 277 us
  matrix products: 161 us -> 16.3 us
  Pallas kernels: 0 us -> 102 us
  local copies, waits for them, and re-layouts: 63.7 us -> 13.2 us
  blocking collectives: 53.2 us -> 95.2 us
  other arithmetic: 38.9 us -> 8.6 us
  starting transfers between devices: 17.9 us -> 40.4 us
    dot_general x37 -> x20, matrix products: 161 us -> 16.3 us  [apply_along(): jnp.tensordot(values, table, axes=([axis], [0]), precision=HIGHEST)]
    all_to_all x2 -> x7, waiting for transfers between devices: 366 us -> 250 us  [the longest x3 127 us: body(): returned.append(exchange(moved))]
    pallas_call x0 -> x9, Pallas kernels: none -> 102 us  [the longest x4 43.9 us: kinetic_across(): pl.pallas_call(partial(across_kernel, planes, first), grid=(vy // by,), i...]
    reduce_scatter x1, waiting for transfers between devices: 44.9 us -> 0.01 us  [body(): share = lax.psum_scatter(density, 'orb', scatter_dimension=1, tiled=True)]
    all_gather x1, waiting for transfers between devices: 43.7 us -> 0.02 us  [body(): gathered = lax.all_gather(rows_back, 'orb', axis=0, tiled=False)]
    all_to_all x1, blocking collectives: 11.8 us -> 54 us  [body(): returned.append(exchange(moved))]
    all_to_all x3 -> x0, local copies, waits for them, and re-layouts: 22.9 us -> none  [the longest x1 15.4 us: body(): lax.all_to_all(moved, 'grid', split_axis=0, concat_axis=4, tiled=True)[0]]
    all_to_all x2 -> x7, starting transfers between devices: 14 us -> 34.4 us  [the longest x4 19.6 us: body(): exchange(kinetic_local(orbitals, layer, grid_count, wz, wy))]
  transfers between devices with their start and end apart: 5 -> 10, of which waited for: 5 -> 8; matrix products, arithmetic and copies ran while one was open for 0% -> 3% of each run, Pallas kernels for 0% -> 12%
where the time goes in v1:
time: 568 us; the launch traced here: 566 us
  waiting for transfers between devices  277 us (49%)
  Pallas kernels  102 us (18%)
  blocking collectives  95.2 us (17%)
  starting transfers between devices  40.4 us (7%)
  matrix products  16.3 us (3%)
  between operations  13.9 us (2%)
  local copies, waits for them, and re-layouts  13.2 us (2%)
  other arithmetic  8.6 us (2%)
    all_to_all x3, waiting for transfers between devices, body(): returned.append(exchange(moved))  127 us
    all_to_all x4, waiting for transfers between devices, body(): exchange(kinetic_local(orbitals, layer, grid_count, wz, wy))  123 us
    all_to_all x1, blocking collectives, body(): returned.append(exchange(moved))  54 us
    pallas_call x4, Pallas kernels, kinetic_across(): pl.pallas_call(partial(across_kernel, planes, first), grid=(vy // by,), i...  43.9 us
    pallas_call x4, Pallas kernels, kinetic_local(): pl.pallas_call(local_kernel, grid=(planes // bx,), in_specs=[pl.BlockSpec...  43.4 us
    all_to_all x1, blocking collectives, poisson_shared(): lax.all_to_all(jnp.stack([real_part, imag_part], 0), ('grid', 'orb'), spl...  30.1 us
    all_to_all x1, waiting for transfers between devices, poisson_shared(): lax.all_to_all(jnp.stack([real_part, imag_part], 0), ('grid', 'orb'), spl...  26.7 us
    all_to_all x4, starting transfers between devices, body(): exchange(kinetic_local(orbitals, layer, grid_count, wz, wy))  19.6 us
  transfers between devices with their start and end apart: 10, of which 8 were waited for; matrix products, arithmetic and copies ran while one was open for 3% of the time, Pallas kernels for 12%

profile of v1, /device:TPU:0, one launch (start us, length us, event | category | flops | bytes accessed | tf_op | source)
XLA Modules:
  0.0 566.3 jit_solution(9622674378359005217)
XLA Ops:
  8.4 10.8 %shard_map.272 = f32[4,2,32,32,128]{4,3,2,1,0:T(8,128)} custom-call(f32[4,2,32,128,128]{4,3,2,1,0:T(8,128)} %psi_ref.7, bf16[2,256,256]{2,1,0:T(8,128)(2,1)S(1)} %copy-done.2, bf16[2,256,256]{2,1,0:T(8,128)(2,1)S(1)} %copy-done), custom_call_target="tpu_custom_call" | custom-call | flops 3221225472 | bytes 8388608 | tf_op jit(solution)/shard_map/pallas_call | solution.py:95
  19.3 5.0 all-to-all-start.1
  24.3 10.8 %shard_map.274 = f32[4,2,32,32,128]{4,3,2,1,0:T(8,128)} custom-call(f32[4,2,32,128,128]{4,3,2,1,0:T(8,128)} %psi_ref.7, bf16[2,256,256]{2,1,0:T(8,128)(2,1)S(1)} %copy-done.3, bf16[2,256,256]{2,1,0:T(8,128)(2,1)S(1)} %copy-done.1), custom_call_target="tpu_custom_call" | custom-call | flops 3221225472 | bytes 8388608 | tf_op jit(solution)/shard_map/pallas_call | solution.py:95
  35.2 38.1 %all-to-all-done.1 = f32[4,2,32,32,128]{4,3,2,1,0:T(8,128)} async-done(((f32[4,2,32,32,128]{4,3,2,1,0:T(8,128)}), f32[4,2,32,32,128]{4,3,2,1,0:T(8,128)}, u32[]{:S(2)}, u32[]{:S(2)}) %all-to-all-start.1) | async-done | bytes 4194336 | tf_op jit(solution)/shard_map/all_to_all | solution.py:279
  73.3 4.8 all-to-all-start.3
  78.1 10.9 %shard_map.273 = f32[4,2,32,32,128]{4,3,2,1,0:T(8,128)} custom-call(f32[4,2,32,128,128]{4,3,2,1,0:T(8,128)} %psi_ref.7, bf16[2,256,256]{2,1,0:T(8,128)(2,1)S(1)} %copy-done.3, bf16[2,256,256]{2,1,0:T(8,128)(2,1)S(1)} %copy-done.1), custom_call_target="tpu_custom_call" | custom-call | flops 3221225472 | bytes 8388608 | tf_op jit(solution)/shard_map/pallas_call | solution.py:95
  89.0 37.3 %all-to-all-done.3 = f32[4,2,32,32,128]{4,3,2,1,0:T(8,128)} async-done(((f32[4,2,32,32,128]{4,3,2,1,0:T(8,128)}), f32[4,2,32,32,128]{4,3,2,1,0:T(8,128)}, u32[]{:S(2)}, u32[]{:S(2)}) %all-to-all-start.3) | async-done | bytes 4194336 | tf_op jit(solution)/shard_map/all_to_all | solution.py:279
  126.3 4.9 all-to-all-start.2
  131.2 10.9 %shard_map.271 = f32[4,2,32,32,128]{4,3,2,1,0:T(8,128)} custom-call(f32[4,2,32,128,128]{4,3,2,1,0:T(8,128)} %psi_ref.7, bf16[2,256,256]{2,1,0:T(8,128)(2,1)S(1)} %copy-done.3, bf16[2,256,256]{2,1,0:T(8,128)(2,1)S(1)} %copy-done.1), custom_call_target="tpu_custom_call" | custom-call | flops 3221225472 | bytes 8388608 | tf_op jit(solution)/shard_map/pallas_call | solution.py:95
  142.1 37.3 %all-to-all-done.2 = f32[4,2,32,32,128]{4,3,2,1,0:T(8,128)} async-done(((f32[4,2,32,32,128]{4,3,2,1,0:T(8,128)}), f32[4,2,32,32,128]{4,3,2,1,0:T(8,128)}, u32[]{:S(2)}, u32[]{:S(2)}) %all-to-all-start.2) | async-done | bytes 4194336 | tf_op jit(solution)/shard_map/all_to_all | solution.py:279
  179.4 4.9 all-to-all-start
  185.2 10.2 %shard_map.275 = (f32[256,32,128]{2,1,0:T(8,128)}, f32[128,32,128]{2,1,0:T(8,128)S(1)}) custom-call(f32[1]{0:T(128)} %get-tuple-element.31.weight_ref, f32[256,32,128]{2,1,0:T(8,128)} %bitcast.3.psi_ref, bf16[2,256,256]{2,1,0:T(8,128)(2,1)S(1)} %copy-done.4), custom_call_target="tpu_custom_call" | custom-call | flops 1610612736 | bytes 12582912 | tf_op jit(solution)/shard_map/pallas_call | solution.py:152
  196.8 11.2 %shard_map.276 = (f32[256,32,128]{2,1,0:T(8,128)}, f32[128,32,128]{2,1,0:T(8,128)S(1)}) custom-call(f32[1]{0:T(128)} %get-tuple-element.32.weight_ref, f32[256,32,128]{2,1,0:T(8,128)} %bitcast.2.psi_ref, bf16[2,256,256]{2,1,0:T(8,128)(2,1)S(1)} %copy-done.4, f32[128,32,128]{2,1,0:T(8,128)} %copy-done.7), custom_call_target="tpu_custom_call" | custom-call | flops 1610612736 | bytes 12582912 | tf_op jit(solution)/shard_map/pallas_call | solution.py:152
  209.3 11.3 %shard_map.277 = (f32[256,32,128]{2,1,0:T(8,128)}, f32[128,32,128]{2,1,0:T(8,128)S(1)}) custom-call(f32[1]{0:T(128)} %get-tuple-element.33.weight_ref, f32[256,32,128]{2,1,0:T(8,128)} %bitcast.1.psi_ref, bf16[2,256,256]{2,1,0:T(8,128)(2,1)S(1)} %copy-done.4, f32[128,32,128]{2,1,0:T(8,128)} %copy-done.6), custom_call_target="tpu_custom_call" | custom-call | flops 1610612736 | bytes 12582912 | tf_op jit(solution)/shard_map/pallas_call | solution.py:152
  222.0 10.5 %all-to-all-done = f32[4,2,32,32,128]{4,3,2,1,0:T(8,128)} async-done(((f32[4,2,32,32,128]{4,3,2,1,0:T(8,128)}), f32[4,2,32,32,128]{4,3,2,1,0:T(8,128)}, u32[]{:S(2)}, u32[]{:S(2)}) %all-to-all-start) | async-done | bytes 4194336 | tf_op jit(solution)/shard_map/all_to_all | solution.py:279
  232.5 11.3 %shard_map.278 = (f32[256,32,128]{2,1,0:T(8,128)}, f32[128,32,128]{2,1,0:T(8,128)}) custom-call(f32[1]{0:T(128)} %get-tuple-element.34.weight_ref, f32[256,32,128]{2,1,0:T(8,128)} %bitcast.psi_ref, bf16[2,256,256]{2,1,0:T(8,128)(2,1)S(1)} %copy-done.4, f32[128,32,128]{2,1,0:T(8,128)} %copy-done.5), custom_call_target="tpu_custom_call" | custom-call | flops 1610612736 | bytes 12582912 | tf_op jit(solution)/shard_map/pallas_call | solution.py:152
  243.8 54.0 %all_to_all.85.refs_0_ = f32[4,2,32,32,128]{4,3,2,1,0:T(8,128)} all-to-all(f32[4,2,32,32,128]{4,3,2,1,0:T(8,128)} %bitcast.114), channel_id=1, replica_groups=mesh['groups'=2,'grid'=4,'orb'=4] {'grid'}, dimensions={0} | all-to-all | bytes 8388608 | tf_op jit(solution)/shard_map/all_to_all | solution.py:287
  297.8 1.7 fusion.25
  299.5 1.7 fusion.27
  305.0 5.7 %all-to-all-start.8 = ((f32[2,128,8,128]{3,2,0,1:T(8,128)}), f32[2,128,8,128]{3,2,0,1:T(8,128)S(1)}, u32[]{:S(2)}, u32[]{:S(2)}) async-start(f32[2,128,8,128]{3,2,0,1:T(8,128)} %copy.88), calls=%async_computation.9 | async-start | bytes 2097152 | tf_op jit(solution)/shard_map/all_to_all | solution.py:232
  310.9 26.7 %all-to-all-done.8 = f32[2,128,8,128]{3,2,0,1:T(8,128)S(1)} async-done(((f32[2,128,8,128]{3,2,0,1:T(8,128)}), f32[2,128,8,128]{3,2,0,1:T(8,128)S(1)}, u32[]{:S(2)}, u32[]{:S(2)}) %all-to-all-start.8) | async-done | bytes 1048608 | tf_op jit(solution)/shard_map/all_to_all | solution.py:232
  344.8 30.1 %all_to_all.86 = f32[2,8,128,128]{3,1,0,2:T(8,128)S(1)} all-to-all(f32[2,8,128,128]{3,1,0,2:T(8,128)S(1)} %copy.96), channel_id=1, replica_groups=mesh['groups'=2,'grid'=4,'orb'=4] {'grid','orb'}, dimensions={2} | all-to-all | bytes 2097152 | tf_op jit(solution)/shard_map/all_to_all | solution.py:253
  374.8 5.1 all-to-all-start.5
  385.6 42.3 %all-to-all-done.5.refs_1_ = f32[4,2,32,32,128]{4,3,2,1,0:T(8,128)} async-done(((f32[4,2,32,32,128]{4,3,2,1,0:T(8,128)}), f32[4,2,32,32,128]{4,3,2,1,0:T(8,128)}, u32[]{:S(2)}, u32[]{:S(2)}) %all-to-all-start.5) | async-done | bytes 4194336 | tf_op jit(solution)/shard_map/all_to_all | solution.py:287
  427.9 11.2 %all_to_all.87 = f32[128,8,128]{2,1,0:T(8,128)S(1)} all-to-all(f32[128,8,128]{2,1,0:T(8,128)S(1)} %copy.106), channel_id=1, replica_groups=mesh['groups'=2,'grid'=4,'orb'=4] {'grid'}, dimensions={0} | all-to-all | bytes 1048576 | tf_op jit(solution)/shard_map/all_to_all | solution.py:291
  439.1 4.8 all-to-all-start.6
  444.9 47.3 %all-to-all-done.6.refs_2_ = f32[4,2,32,32,128]{4,3,2,1,0:T(8,128)} async-done(((f32[4,2,32,32,128]{4,3,2,1,0:T(8,128)}), f32[4,2,32,32,128]{4,3,2,1,0:T(8,128)}, u32[]{:S(2)}, u32[]{:S(2)}) %all-to-all-start.6) | async-done | bytes 4194336 | tf_op jit(solution)/shard_map/all_to_all | solution.py:287
  492.1 4.9 all-to-all-start.7
  497.1 2.0 copy.108
  499.3 8.4 %fusion.11 = (f32[32,128,128]{2,1,0:T(8,128)}, f32[32,128,128]{2,1,0:T(8,128)S(1)}) fusion(f32[32,128,128]{2,1,0:T(8,128)S(1)} %copy-done.8, f32[32,4,4,8,128]{4,3,2,1,0:T(8,128)S(1)} %copy.108), kind=kLoop, calls=%fused_computation.24 | loop fusion | flops 1048576 | bytes 8388608 | tf_op jit(solution)/shard_map/sin | solution.py:296
  507.7 37.6 %all-to-all-done.7.refs_3_ = f32[4,2,32,32,128]{4,3,2,1,0:T(8,128)} async-done(((f32[4,2,32,32,128]{4,3,2,1,0:T(8,128)}), f32[4,2,32,32,128]{4,3,2,1,0:T(8,128)}, u32[]{:S(2)}, u32[]{:S(2)}) %all-to-all-start.7) | async-done | bytes 4194336 | tf_op jit(solution)/shard_map/all_to_all | solution.py:287
  545.2 14.3 %shard_map.279 = f32[4,2,32,128,128]{4,3,2,1,0:T(8,128)} custom-call(f32[4,2,32,32,128]{4,3,2,1,0:T(8,128)} %all_to_all.85.refs_0_, f32[4,2,32,32,128]{4,3,2,1,0:T(8,128)} %all-to-all-done.5.refs_1_, f32[4,2,32,32,128]{4,3,2,1,0:T(8,128)} %all-to-all-done.6.refs_2_, f32[4,2,32,32,128]{4,3,2,1,0:T(8,128)} %all-to-all-done.7.refs_3_, ...), custom_call_target="tpu_custom_call" | custom-call | tf_op jit(solution)/shard_map/pallas_call | solution.py:192
  (72 shorter events, 24.6 us)
Async XLA Ops:
  6.5 0.9 copy-start
  7.5 0.9 copy-start.2
  19.3 5.0 copy-start.1
  19.3 5.0 copy-start.3
  19.3 54.0 %all-to-all-start.1 = ((f32[4,2,32,32,128]{4,3,2,1,0:T(8,128)}), f32[4,2,32,32,128]{4,3,2,1,0:T(8,128)}, u32[]{:S(2)}, u32[]{:S(2)}) async-start(f32[4,2,32,32,128]{4,3,2,1,0:T(8,128)} %shard_map.272), calls=%async_computation.1 | async-start | bytes 8388608 | tf_op jit(solution)/shard_map/all_to_all | solution.py:279
  73.3 53.1 %all-to-all-start.3 = ((f32[4,2,32,32,128]{4,3,2,1,0:T(8,128)}), f32[4,2,32,32,128]{4,3,2,1,0:T(8,128)}, u32[]{:S(2)}, u32[]{:S(2)}) async-start(f32[4,2,32,32,128]{4,3,2,1,0:T(8,128)} %shard_map.274), calls=%async_computation.3 | async-start | bytes 8388608 | tf_op jit(solution)/shard_map/all_to_all | solution.py:279
  126.3 53.1 %all-to-all-start.2 = ((f32[4,2,32,32,128]{4,3,2,1,0:T(8,128)}), f32[4,2,32,32,128]{4,3,2,1,0:T(8,128)}, u32[]{:S(2)}, u32[]{:S(2)}) async-start(f32[4,2,32,32,128]{4,3,2,1,0:T(8,128)} %shard_map.273), calls=%async_computation.2 | async-start | bytes 8388608 | tf_op jit(solution)/shard_map/all_to_all | solution.py:279
  142.1 42.4 %copy-start.14 = (f32[16]{0:T(128)S(1)}, f32[16]{0:T(128)}, u32[]{:S(2)}) copy-start(f32[16]{0:T(128)} %param.31) | copy-start | bytes 196
  142.1 43.1 %copy-start.4 = (bf16[2,256,256]{2,1,0:T(8,128)(2,1)S(1)}, bf16[2,256,256]{2,1,0:T(8,128)(2,1)}, u32[]{:S(2)}) copy-start(bf16[2,256,256]{2,1,0:T(8,128)(2,1)} %constant.48.clone.wx_ref) | copy-start | bytes 786436
  179.4 53.1 %all-to-all-start = ((f32[4,2,32,32,128]{4,3,2,1,0:T(8,128)}), f32[4,2,32,32,128]{4,3,2,1,0:T(8,128)}, u32[]{:S(2)}, u32[]{:S(2)}) async-start(f32[4,2,32,32,128]{4,3,2,1,0:T(8,128)} %shard_map.271), calls=%async_computation | async-start | bytes 8388608 | tf_op jit(solution)/shard_map/all_to_all | solution.py:279
  184.3 113.5 %reduce-scatter.2.cloned.1.call-start = ((), (), s32[]{:S(2)}) async-start(), calls=%async_computation.12 | async-start | bytes 2621440 | tf_op jit(solution)/shard_map/reduce_scatter | solution.py:288
  195.4 1.4 copy-start.7
  208.0 1.4 copy-start.6
  220.6 1.4 copy-start.5
  243.8 54.0 %copy-start.11 = (f32[128,128,1]{1,0,2:T(8,128)S(1)}, f32[128,128,1]{1,0,2:T(8,128)}, u32[]{:S(2)}) copy-start(f32[128,128,1]{1,0,2:T(8,128)} %constant.60) | copy-start | bytes 196612
  243.8 55.7 %copy-start.12 = (f32[128,128,1]{1,0,2:T(8,128)S(1)}, f32[128,128,1]{1,0,2:T(8,128)}, u32[]{:S(2)}) copy-start(f32[128,128,1]{1,0,2:T(8,128)} %constant.59) | copy-start | bytes 196612
  302.9 7.8 %copy-start.13 = (f32[128]{0:T(128)S(1)}, f32[128]{0:T(128)}, u32[]{:S(2)}) copy-start(f32[128]{0:T(128)} %constant.51.clone) | copy-start | bytes 1540
  305.0 32.5 %all-to-all-start.8 = ((f32[2,128,8,128]{3,2,0,1:T(8,128)}), f32[2,128,8,128]{3,2,0,1:T(8,128)S(1)}, u32[]{:S(2)}, u32[]{:S(2)}) async-start(f32[2,128,8,128]{3,2,0,1:T(8,128)} %copy.88), calls=%async_computation.9 | async-start | bytes 2097152 | tf_op jit(solution)/shard_map/all_to_all | solution.py:232
  337.7 4.2 copy-start.9
  338.7 3.8 copy-start.10
  374.8 53.1 %all-to-all-start.5 = ((f32[4,2,32,32,128]{4,3,2,1,0:T(8,128)}), f32[4,2,32,32,128]{4,3,2,1,0:T(8,128)}, u32[]{:S(2)}, u32[]{:S(2)}) async-start(f32[4,2,32,32,128]{4,3,2,1,0:T(8,128)} %bitcast.113), calls=%async_computation.6 | async-start | bytes 8388608 | tf_op jit(solution)/shard_map/all_to_all | solution.py:287
  439.1 53.1 %all-to-all-start.6 = ((f32[4,2,32,32,128]{4,3,2,1,0:T(8,128)}), f32[4,2,32,32,128]{4,3,2,1,0:T(8,128)}, u32[]{:S(2)}, u32[]{:S(2)}) async-start(f32[4,2,32,32,128]{4,3,2,1,0:T(8,128)} %bitcast.112), calls=%async_computation.7 | async-start | bytes 8388608 | tf_op jit(solution)/shard_map/all_to_all | solution.py:287
  443.9 53.1 %all-gather.2.cloned.1.call-start = ((), (), s32[]{:S(2)}) async-start(), calls=%async_computation.13 | async-start | bytes 2621440 | tf_op jit(solution)/shard_map/all_gather | solution.py:292
  492.1 53.1 %all-to-all-start.7 = ((f32[4,2,32,32,128]{4,3,2,1,0:T(8,128)}), f32[4,2,32,32,128]{4,3,2,1,0:T(8,128)}, u32[]{:S(2)}, u32[]{:S(2)}) async-start(f32[4,2,32,32,128]{4,3,2,1,0:T(8,128)} %bitcast.111), calls=%async_computation.8 | async-start | bytes 8388608 | tf_op jit(solution)/shard_map/all_to_all | solution.py:287
  497.0 2.2 copy-start.8
Sparse Core Ops, SparseCore 0:
  243.9 44.6 reduce-scatter.1
  446.3 44.6 all-gather.1
